TPU v7x, 32 devices: a whole 2x2x4 slice. The times are simulated.
32 devices in a mesh: seq: 8 (over z, x), head: 4 (over y, core).
Axes of the slice: x: 2, y: 2, z: 4, core: 2. Of those that a mesh axis runs over, the one named last changes fastest.
Arguments:
- queries: bfloat16 [1024, 3072], P('seq', 'head'), may hold values from -8 to 8
- latents: bfloat16 [1024, 576], P('seq'), may hold values from -8 to 8
- key_up: bfloat16 [512, 2048], P(None, 'head'), may hold values from -0.25 to 0.25
- value_up: bfloat16 [512, 2048], P(None, 'head'), may hold values from -0.25 to 0.25
- out_grad: bfloat16 [1024, 2048], P('seq', 'head'), may hold values from -48 to 48
- positions: int32 [1024], P('seq'), may hold values from 0 to 1023, as said below
Outputs:
- query_grad: bfloat16 [1024, 3072], P('seq', 'head')
- latent_grad: float32 [1024, 576], P('seq')
- key_up_grad: float32 [512, 2048], P(None, 'head')
- value_up_grad: float32 [512, 2048], P(None, 'head')
Inputs may be any that keep to these rules, and one draw needn't show every extreme that they name: Every position from 0 to 1023 occurs once; positions come in stripes of 128 consecutive positions in ascending order, each stripe whole within the rows of one device.
All inputs are finite; a program needn't handle non-finite values.
Results may differ from a plain program's by a relative error of at most 0.0084.
Values may be sent and summed in bfloat16 or wider, within the bound.
A program may use at most 64 MiB of HBM per device.

v0:
```python
import math
import jax
import jax.numpy as jnp
from jax import lax
from jax.sharding import PartitionSpec as P

D_LAT = 512
D_ROPE = 64
D_NOPE = 128
D_V = 128
NEG = -1e30


def shifted(value, axis, steps):
    count = lax.axis_size(axis)
    pairs = [(source, (source + steps) % count) for source in range(count)]
    return lax.ppermute(value, axis, pairs)


def up_project(block, key_up, value_up):
    compressed = block[:, :D_LAT]
    key_nope = jnp.dot(compressed, key_up, preferred_element_type=jnp.float32).astype(jnp.bfloat16)
    values = jnp.dot(compressed, value_up, preferred_element_type=jnp.float32).astype(jnp.bfloat16)
    return (key_nope, block[:, D_LAT:], values)


def split_heads(queries, out_grad, key_nope, values):
    heads = key_nope.shape[1] // D_NOPE
    shaped = queries.reshape(queries.shape[0], heads, D_NOPE + D_ROPE)
    grads = out_grad.reshape(out_grad.shape[0], heads, D_V)
    key3 = key_nope.reshape(key_nope.shape[0], heads, D_NOPE)
    value3 = values.reshape(values.shape[0], heads, D_V)
    return (shaped[:, :, :D_NOPE], shaped[:, :, D_NOPE:], grads, key3, value3)


def scores_of(q_nope, q_rope, key3, rope_keys, query_pos, key_pos):
    scale = 1.0 / math.sqrt(D_NOPE + D_ROPE)
    raw = jnp.einsum("bhd,khd->hbk", q_nope, key3, preferred_element_type=jnp.float32)
    raw = raw + jnp.einsum("bhd,kd->hbk", q_rope, rope_keys, preferred_element_type=jnp.float32)
    visible = (key_pos[None, :] <= query_pos[:, None])[None]
    return (raw * scale, visible)


def forward_update(stats, queries, out_grad, query_pos, key_nope, rope_keys, values, key_pos):
    top, total, weighted = stats
    q_nope, q_rope, grads, key3, value3 = split_heads(queries, out_grad, key_nope, values)
    scores, visible = scores_of(q_nope, q_rope, key3, rope_keys, query_pos, key_pos)
    dprobs = jnp.einsum("bhd,khd->hbk", grads, value3, preferred_element_type=jnp.float32)
    masked = jnp.where(visible, scores, NEG)
    new_top = jnp.maximum(top, jnp.max(masked, axis=2))
    weights = jnp.exp(jnp.where(visible, scores - new_top[:, :, None], NEG))
    fade = jnp.exp(top - new_top)
    total = total * fade + jnp.sum(weights, axis=2)
    weighted = weighted * fade + jnp.sum(weights * dprobs, axis=2)
    return (new_top, total, weighted)


def backward_terms(queries, out_grad, query_pos, lse, delta, key_nope, rope_keys, values, key_pos):
    scale = 1.0 / math.sqrt(D_NOPE + D_ROPE)
    q_nope, q_rope, grads, key3, value3 = split_heads(queries, out_grad, key_nope, values)
    scores, visible = scores_of(q_nope, q_rope, key3, rope_keys, query_pos, key_pos)
    probs = jnp.exp(jnp.where(visible, scores - lse[:, :, None], NEG))
    dprobs = jnp.einsum("bhd,khd->hbk", grads, value3, preferred_element_type=jnp.float32)
    dscore = (probs * (dprobs - delta[:, :, None]) * scale).astype(jnp.bfloat16)
    probs16 = probs.astype(jnp.bfloat16)
    grad_nope = jnp.einsum("hbk,khd->bhd", dscore, key3, preferred_element_type=jnp.float32)
    grad_rope = jnp.einsum("hbk,kd->bhd", dscore, rope_keys, preferred_element_type=jnp.float32)
    q_grad = jnp.concatenate([grad_nope, grad_rope], axis=2).reshape(queries.shape[0], -1)
    key_part = jnp.einsum("hbk,bhd->khd", dscore, q_nope, preferred_element_type=jnp.float32)
    value_part = jnp.einsum("hbk,bhd->khd", probs16, grads, preferred_element_type=jnp.float32)
    rope_part = jnp.einsum("hbk,bhd->kd", dscore, q_rope, preferred_element_type=jnp.float32)
    key_rows = key3.shape[0]
    part = jnp.concatenate(
        [key_part.reshape(key_rows, -1), value_part.reshape(key_rows, -1), rope_part], axis=1
    )
    return (q_grad, part)


def shards(queries, latents, key_up, value_up, out_grad, positions):
    rows = queries.shape[0]
    heads = key_up.shape[1] // D_NOPE
    qcols = queries.shape[1]
    nseq = lax.axis_size("seq")
    here = lax.axis_index("seq")
    every_pos = lax.all_gather(positions, "seq", axis=0, tiled=True)
    part_width = heads * (D_NOPE + D_V) + D_ROPE

    def owner_start(step):
        return (here - step) % nseq * rows

    def owner_pos(step):
        return lax.dynamic_slice_in_dim(every_pos, owner_start(step), rows, 0)

    start_stats = (
        jnp.full((heads, rows), NEG, jnp.float32),
        jnp.zeros((heads, rows), jnp.float32),
        jnp.zeros((heads, rows), jnp.float32),
    )
    zero_grads = jnp.zeros((rows, part_width), jnp.float32)
    zero_query = jnp.zeros((rows, qcols), jnp.float32)

    def fold_block(stats, block, start):
        key_nope, rope_keys, values = up_project(block, key_up, value_up)
        key_pos = lax.dynamic_slice_in_dim(every_pos, start, block.shape[0], 0)
        return forward_update(
            stats, queries, out_grad, positions, key_nope, rope_keys, values, key_pos
        )

    def grad_block(block, grads, q_acc, step, lse, delta):
        key_nope, rope_keys, values = up_project(block, key_up, value_up)
        q_grad, part = backward_terms(
            queries, out_grad, positions, lse, delta, key_nope, rope_keys, values, owner_pos(step)
        )
        return (grads + part, q_acc + q_grad)

    gathered = lax.all_gather(latents, "seq", axis=0, tiled=True)
    count = gathered.shape[0]
    width = math.gcd(count, 512)

    def turn(index, carry):
        block = lax.dynamic_slice_in_dim(gathered, index * width, width, 0)
        return fold_block(carry, block, index * width)

    top, total, weighted = lax.fori_loop(0, count // width, turn, start_stats)
    lse = top + jnp.log(total)
    delta = weighted / total

    def kept_turn(step, carry):
        grads, q_acc = carry
        block = lax.dynamic_slice_in_dim(gathered, owner_start(step), rows, 0)
        grads, q_acc = grad_block(block, grads, q_acc, step, lse, delta)
        grads = shifted(grads, "seq", 1)
        return (grads, q_acc)

    grads, q_acc = lax.fori_loop(0, nseq - 1, kept_turn, (zero_grads, zero_query))
    last_block = lax.dynamic_slice_in_dim(gathered, owner_start(nseq - 1), rows, 0)
    grads, q_acc = grad_block(last_block, grads, q_acc, nseq - 1, lse, delta)
    key_grads = shifted(grads, "seq", 1)
    split_one = heads * D_NOPE
    split_two = split_one + heads * D_V
    key_grad = key_grads[:, :split_one]
    value_grad = key_grads[:, split_one:split_two]
    high = lax.Precision.HIGHEST
    key_up32 = key_up.astype(jnp.float32)
    value_up32 = value_up.astype(jnp.float32)
    inner = (((1,), (1,)), ((), ()))
    folded = lax.dot_general(key_grad, key_up32, inner, precision=high)
    folded = folded + lax.dot_general(value_grad, value_up32, inner, precision=high)
    latent_part = jnp.concatenate([folded, key_grads[:, split_two:]], axis=1)
    latent_grad = lax.psum(latent_part, "head")
    compressed = latents[:, :D_LAT].astype(jnp.float32)
    outer = (((0,), (0,)), ((), ()))
    key_term = lax.dot_general(compressed, key_grad, outer, precision=high)
    value_term = lax.dot_general(compressed, value_grad, outer, precision=high)
    key_up_grad, value_up_grad = lax.psum((key_term, value_term), "seq")
    return (q_acc.astype(jnp.bfloat16), latent_grad, key_up_grad, value_up_grad)


def solution(mesh):
    in_specs = (
        P("seq", "head"),
        P("seq", None),
        P(None, "head"),
        P(None, "head"),
        P("seq", "head"),
        P("seq"),
    )
    out_specs = (P("seq", "head"), P("seq", None), P(None, "head"), P(None, "head"))
    return jax.shard_map(shards, mesh=mesh, in_specs=in_specs, out_specs=out_specs, check_vma=False)
```

profile of v0, /device:TPU:0, one launch (start us, length us, event | category | flops | bytes accessed | tf_op | source)
XLA Modules:
  0.0 364.3 jit_solution(10623151957692037776)
XLA Ops:
  8.1 1.0 copy.106
  9.1 1.1 copy.105
  10.2 22.5 %all-gather = s32[8,1,128]{2,1,0:T(1,128)S(1)} all-gather(s32[1,1,128]{2,1,0:T(1,128)} %bitcast.257), channel_id=1, replica_groups=mesh['seq'=8,'head'=4] {'seq'}, dimensions={0}, use_global_device_ids=true | all-gather | bytes 4608 | tf_op jit(solution)/shard_map/all_gather | solution.py:85
  33.5 19.7 %all-gather.3.cloned.1.call-done = bf16[1024,576]{0,1:T(8,128)(2,1)} async-done(((bf16[128,576]{0,1:T(8,128)(2,1)}), bf16[1024,576]{0,1:T(8,128)(2,1)}) %all-gather.3.cloned.1.call-update) | async-done | bytes 1179664 | tf_op jit(solution)/shard_map/all_gather | solution.py:116
  53.2 1.4 convolution_convert_fusion.5
  54.8 7.6 %while.36 = (s32[]{:T(128)}, f32[4,128]{1,0:T(4,128)S(1)}, f32[4,128]{1,0:T(4,128)S(1)}, f32[4,128]{1,0:T(4,128)S(1)}, s32[1024]{0:T(1024)S(1)}, /*index=5*/s32[...) while((s32[]{:T(128)}, f32[4,128]{1,0:T(4,128)S(1)}, ...), condition=%wide.region_4.5_spmd.clone, body=%wide.region_0.4_spmd.clone.sunk | while | flops 708120064 | bytes 14854930 | solution.py:124
  55.0 1.6 convolution_convert_fusion.10
  58.8 1.6 convolution_convert_fusion.10
  62.4 0.9 convolution_bitcast_fusion.12
  63.8 1.2 fusion.47
  66.3 135.5 %while.37 = (s32[]{:T(128)}, f32[128,1088]{0,1:T(8,128)S(1)}, f32[128,768]{0,1:T(8,128)S(1)}, s32[]{:T(128)}, s32[1024]{0:T(1024)S(1)}, /*index=5*/s32[128]{0:T(...) while((s32[]{:T(128)}, f32[128,1088]{0,1:T(8,128)S(1)}, ...), condition=%wide.region_6.7_spmd.clone, body=%wide.region_5.6_spmd.clone.sunk | while | flops 244719632 | bytes 11737526 | solution.py:135
  66.4 1.2 fusion.162
  67.6 1.2 convolution_convert_fusion.11
  69.0 0.9 convolution_bitcast_fusion.21
  71.8 1.4 collective-permute-start
  74.4 12.3 %collective-permute-done = f32[128,1088]{0,1:T(8,128)S(1)} collective-permute-done((f32[128,1088]{0,1:T(8,128)}, f32[128,1088]{0,1:T(8,128)S(1)}, u32[]{:S(2)}, u32[]{:S(2)}) %collective-permute-start) | collective-permute-done | bytes 557088 | tf_op jit(solution)/shard_map/while/body/eval_jaxpr/ppermute | solution.py:17
  86.7 1.2 fusion.162
  87.9 1.2 convolution_convert_fusion.11
  89.3 0.9 convolution_bitcast_fusion.21
  92.1 1.2 collective-permute-start
  94.5 12.9 %collective-permute-done = f32[128,1088]{0,1:T(8,128)S(1)} collective-permute-done((f32[128,1088]{0,1:T(8,128)}, f32[128,1088]{0,1:T(8,128)S(1)}, u32[]{:S(2)}, u32[]{:S(2)}) %collective-permute-start) | collective-permute-done | bytes 557088 | tf_op jit(solution)/shard_map/while/body/eval_jaxpr/ppermute | solution.py:17
  107.5 1.2 fusion.162
  108.6 1.2 convolution_convert_fusion.11
  110.0 0.9 convolution_bitcast_fusion.21
  114.0 13.2 %collective-permute-done = f32[128,1088]{0,1:T(8,128)S(1)} collective-permute-done((f32[128,1088]{0,1:T(8,128)}, f32[128,1088]{0,1:T(8,128)S(1)}, u32[]{:S(2)}, u32[]{:S(2)}) %collective-permute-start) | collective-permute-done | bytes 557088 | tf_op jit(solution)/shard_map/while/body/eval_jaxpr/ppermute | solution.py:17
  127.3 1.2 fusion.162
  128.5 1.2 convolution_convert_fusion.11
  129.9 0.9 convolution_bitcast_fusion.21
  133.9 12.4 %collective-permute-done = f32[128,1088]{0,1:T(8,128)S(1)} collective-permute-done((f32[128,1088]{0,1:T(8,128)}, f32[128,1088]{0,1:T(8,128)S(1)}, u32[]{:S(2)}, u32[]{:S(2)}) %collective-permute-start) | collective-permute-done | bytes 557088 | tf_op jit(solution)/shard_map/while/body/eval_jaxpr/ppermute | solution.py:17
  146.3 1.2 fusion.162
  147.5 1.2 convolution_convert_fusion.11
  148.9 0.9 convolution_bitcast_fusion.21
  152.9 11.5 %collective-permute-done = f32[128,1088]{0,1:T(8,128)S(1)} collective-permute-done((f32[128,1088]{0,1:T(8,128)}, f32[128,1088]{0,1:T(8,128)S(1)}, u32[]{:S(2)}, u32[]{:S(2)}) %collective-permute-start) | collective-permute-done | bytes 557088 | tf_op jit(solution)/shard_map/while/body/eval_jaxpr/ppermute | solution.py:17
  164.5 1.2 fusion.162
  165.7 1.2 convolution_convert_fusion.11
  171.1 11.3 %collective-permute-done = f32[128,1088]{0,1:T(8,128)S(1)} collective-permute-done((f32[128,1088]{0,1:T(8,128)}, f32[128,1088]{0,1:T(8,128)S(1)}, u32[]{:S(2)}, u32[]{:S(2)}) %collective-permute-start) | collective-permute-done | bytes 557088 | tf_op jit(solution)/shard_map/while/body/eval_jaxpr/ppermute | solution.py:17
  182.4 1.2 fusion.162
  183.6 1.2 convolution_convert_fusion.11
  189.0 12.8 %collective-permute-done = f32[128,1088]{0,1:T(8,128)S(1)} collective-permute-done((f32[128,1088]{0,1:T(8,128)}, f32[128,1088]{0,1:T(8,128)S(1)}, u32[]{:S(2)}, u32[]{:S(2)}) %collective-permute-start) | collective-permute-done | bytes 557088 | tf_op jit(solution)/shard_map/while/body/eval_jaxpr/ppermute | solution.py:17
  201.8 1.0 maximum_add_fusion.1
  202.9 12.2 %collective-permute-done.1 = f32[128,1088]{0,1:T(8,128)S(1)} collective-permute-done((f32[128,1088]{0,1:T(8,128)S(1)}, f32[128,1088]{0,1:T(8,128)S(1)}, u32[]{:S(2)}, u32[]{:S(2)}) %collective-permute-start.1) | collective-permute-done | bytes 557088 | tf_op jit(solution)/shard_map/ppermute | solution.py:17
  217.4 1.6 convolution_bitcast_fusion.9
  219.0 1.5 convolution_bitcast_fusion.8
  222.7 24.6 %all-reduce.4.cloned.1.call-done = f32[128,576]{1,0:T(8,128)} async-done(((f32[128,576]{1,0:T(8,128)}), f32[128,576]{1,0:T(8,128)}) %all-reduce.4.cloned.1.call-update) | async-done | bytes 294928 | tf_op jit(solution)/shard_map/psum | solution.py:150
  247.3 1.8 copy.123
  249.1 104.7 %all-reduce.6.cloned.1.call-done = (f32[512,512]{0,1:T(8,128)}, f32[512,512]{0,1:T(8,128)}) async-done(((f32[512,512]{0,1:T(8,128)}, f32[512,512]{0,1:T(8,128)}), (f32[512,512]{0,1:T(8,128)}, f32[512,512]{0,1:T(8,128)})) %all-reduce.6.cloned.1.call-update) | async-done | bytes 2097168 | tf_op jit(solution)/shard_map/psum | solution.py:155
  353.9 2.6 copy.124
  356.5 1.3 copy.125
  (166 shorter events, 37.2 us)
Async XLA Ops:
  7.2 47.6 %copy-start.5 = (bf16[128,512]{1,0:T(8,128)(2,1)S(1)}, bf16[128,512]{1,0:T(8,128)(2,1)}, u32[]{:S(2)}) copy-start(bf16[128,512]{1,0:T(8,128)(2,1)} %param.14) | copy-start | bytes 393220
  7.2 47.6 %copy-start.6 = (s32[128]{0:T(128)S(1)}, s32[128]{0:T(128)}, u32[]{:S(2)}) copy-start(s32[128]{0:T(128)} %param.15) | copy-start | bytes 1540
  7.2 47.6 %copy-start.1 = (bf16[512,512]{1,0:T(8,128)(2,1)S(1)}, bf16[512,512]{1,0:T(8,128)(2,1)}, u32[]{:S(2)}) copy-start(bf16[512,512]{1,0:T(8,128)(2,1)} %param.12) | copy-start | bytes 1572868
  7.2 47.6 %copy-start = (bf16[512,512]{1,0:T(8,128)(2,1)S(1)}, bf16[512,512]{1,0:T(8,128)(2,1)}, u32[]{:S(2)}) copy-start(bf16[512,512]{1,0:T(8,128)(2,1)} %param.13) | copy-start | bytes 1572868
  7.2 46.0 %all-gather.3.cloned.1.call-start = ((), (), s32[]{:S(2)}) async-start(), calls=%async_computation | async-start | bytes 1327104 | tf_op jit(solution)/shard_map/all_gather | solution.py:116
  7.9 239.3 %all-reduce.4.cloned.1.call-start = ((), (), s32[]{:S(2)}) async-start(), calls=%async_computation.1 | async-start | bytes 655360 | tf_op jit(solution)/shard_map/psum | solution.py:150
  54.8 1.9 copy-start.2
  58.6 1.9 copy-start.2
  71.8 14.8 %collective-permute-start = (f32[128,1088]{0,1:T(8,128)}, f32[128,1088]{0,1:T(8,128)S(1)}, u32[]{:S(2)}, u32[]{:S(2)}) collective-permute-start(f32[128,1088]{0,1:T(8,128)} %maximum_add_fusion.3), channel_id=1, source_target_pairs={{0,4},{4,8},{8,12},{12,16},{16,20},{20,24},{24,28},{28,0},{1,5},{5... | collective-permute-start | bytes 1671176 | tf_op jit(solution)/shard_map/while/body/eval_jaxpr/ppermute | solution.py:17
  92.1 15.2 %collective-permute-start = (f32[128,1088]{0,1:T(8,128)}, f32[128,1088]{0,1:T(8,128)S(1)}, u32[]{:S(2)}, u32[]{:S(2)}) collective-permute-start(f32[128,1088]{0,1:T(8,128)} %maximum_add_fusion.3), channel_id=1, source_target_pairs={{0,4},{4,8},{8,12},{12,16},{16,20},{20,24},{24,28},{28,0},{1,5},{5... | collective-permute-start | bytes 1671176 | tf_op jit(solution)/shard_map/while/body/eval_jaxpr/ppermute | solution.py:17
  112.9 14.4 %collective-permute-start = (f32[128,1088]{0,1:T(8,128)}, f32[128,1088]{0,1:T(8,128)S(1)}, u32[]{:S(2)}, u32[]{:S(2)}) collective-permute-start(f32[128,1088]{0,1:T(8,128)} %maximum_add_fusion.3), channel_id=1, source_target_pairs={{0,4},{4,8},{8,12},{12,16},{16,20},{20,24},{24,28},{28,0},{1,5},{5... | collective-permute-start | bytes 1671176 | tf_op jit(solution)/shard_map/while/body/eval_jaxpr/ppermute | solution.py:17
  132.7 13.5 %collective-permute-start = (f32[128,1088]{0,1:T(8,128)}, f32[128,1088]{0,1:T(8,128)S(1)}, u32[]{:S(2)}, u32[]{:S(2)}) collective-permute-start(f32[128,1088]{0,1:T(8,128)} %maximum_add_fusion.3), channel_id=1, source_target_pairs={{0,4},{4,8},{8,12},{12,16},{16,20},{20,24},{24,28},{28,0},{1,5},{5... | collective-permute-start | bytes 1671176 | tf_op jit(solution)/shard_map/while/body/eval_jaxpr/ppermute | solution.py:17
  151.7 12.7 %collective-permute-start = (f32[128,1088]{0,1:T(8,128)}, f32[128,1088]{0,1:T(8,128)S(1)}, u32[]{:S(2)}, u32[]{:S(2)}) collective-permute-start(f32[128,1088]{0,1:T(8,128)} %maximum_add_fusion.3), channel_id=1, source_target_pairs={{0,4},{4,8},{8,12},{12,16},{16,20},{20,24},{24,28},{28,0},{1,5},{5... | collective-permute-start | bytes 1671176 | tf_op jit(solution)/shard_map/while/body/eval_jaxpr/ppermute | solution.py:17
  169.9 12.4 %collective-permute-start = (f32[128,1088]{0,1:T(8,128)}, f32[128,1088]{0,1:T(8,128)S(1)}, u32[]{:S(2)}, u32[]{:S(2)}) collective-permute-start(f32[128,1088]{0,1:T(8,128)} %maximum_add_fusion.3), channel_id=1, source_target_pairs={{0,4},{4,8},{8,12},{12,16},{16,20},{20,24},{24,28},{28,0},{1,5},{5... | collective-permute-start | bytes 1671176 | tf_op jit(solution)/shard_map/while/body/eval_jaxpr/ppermute | solution.py:17
  187.8 14.0 %collective-permute-start = (f32[128,1088]{0,1:T(8,128)}, f32[128,1088]{0,1:T(8,128)S(1)}, u32[]{:S(2)}, u32[]{:S(2)}) collective-permute-start(f32[128,1088]{0,1:T(8,128)} %maximum_add_fusion.3), channel_id=1, source_target_pairs={{0,4},{4,8},{8,12},{12,16},{16,20},{20,24},{24,28},{28,0},{1,5},{5... | collective-permute-start | bytes 1671176 | tf_op jit(solution)/shard_map/while/body/eval_jaxpr/ppermute | solution.py:17
  202.8 12.3 %collective-permute-start.1 = (f32[128,1088]{0,1:T(8,128)S(1)}, f32[128,1088]{0,1:T(8,128)S(1)}, u32[]{:S(2)}, u32[]{:S(2)}) collective-permute-start(f32[128,1088]{0,1:T(8,128)S(1)} %maximum_add_fusion.1), channel_id=1, source_target_pairs={{0,4},{4,8},{8,12},{12,16},{16,20},{20,24},{24,28},{28,0},{1,5},{5... | collective-permute-start | bytes 1671176 | tf_op jit(solution)/shard_map/ppermute | solution.py:17
  215.9 1.6 copy-start.3
  217.4 136.5 %all-reduce.6.cloned.1.call-start = ((), (), s32[]{:S(2)}) async-start(), calls=%async_computation.2 | async-start | bytes 4194304 | tf_op jit(solution)/shard_map/psum | solution.py:155
  353.9 2.6 copy-start.4
Sparse Core Ops, SparseCore 0:
  10.1 43.1 all-gather.2
  217.5 29.7 all-reduce.3
  251.5 102.2 all-reduce.5
where the time goes:
time: 366 us; the launch traced here: 364 us
  waiting for transfers between devices  248 us (68%)
  matrix products  54.3 us (15%)
  blocking collectives  22.5 us (6%)
  between operations  14.1 us (4%)
  other arithmetic  11.5 us (3%)
  local copies, waits for them, and re-layouts  10.1 us (3%)
    psum x1, waiting for transfers between devices, shards(): key_up_grad, value_up_grad = lax.psum((key_term, value_term), 'seq')  105 us
    ppermute x8, waiting for transfers between devices, shifted(): return lax.ppermute(value, axis, pairs)  98.6 us
    psum x1, waiting for transfers between devices, shards(): latent_grad = lax.psum(latent_part, 'head')  24.6 us
    all_gather x1, blocking collectives, shards(): every_pos = lax.all_gather(positions, 'seq', axis=0, tiled=True)  22.5 us
    all_gather x1, waiting for transfers between devices, shards(): gathered = lax.all_gather(latents, 'seq', axis=0, tiled=True)  19.7 us
    dot_general x10, matrix products, up_project(): jnp.dot(compressed, value_up, preferred_element_type=jnp.float32)  12.5 us
    dot_general x10, matrix products, up_project(): jnp.dot(compressed, key_up, preferred_element_type=jnp.float32)  10.5 us
    dot_general x10, matrix products, scores_of(): jnp.einsum('bhd,kd->hbk', q_rope, rope_keys, preferred_element_type=jnp.f...  8.11 us
  transfers between devices with their start and end apart: 11, of which 11 were waited for; matrix products, arithmetic and copies ran while one was open for 5% of the time, Pallas kernels for 0%

commit v1 on v0

--- a/solution.py
+++ b/solution.py
@@ -147,7 +147,7 @@
     folded = lax.dot_general(key_grad, key_up32, inner, precision=high)
     folded = folded + lax.dot_general(value_grad, value_up32, inner, precision=high)
     latent_part = jnp.concatenate([folded, key_grads[:, split_two:]], axis=1)
-    latent_grad = lax.psum(latent_part, "head")
+    latent_grad = jnp.sum(lax.all_gather(latent_part, "head"), axis=0)
     compressed = latents[:, :D_LAT].astype(jnp.float32)
     outer = (((0,), (0,)), ((), ()))
     key_term = lax.dot_general(compressed, key_grad, outer, precision=high)

time: 366 us -> 351 us (0.959)
  waiting for transfers between devices: 248 us -> 233 us
    psum x1 -> x0, waiting for transfers between devices: 24.6 us -> none  [shards(): latent_grad = lax.psum(latent_part, 'head')]
    all_gather x0 -> x1, waiting for transfers between devices: none -> 10.2 us  [shards(): latent_grad = jnp.sum(lax.all_gather(latent_part, 'head'), axis=0)]
where the time goes in v1:
time: 351 us; the launch traced here: 350 us
  waiting for transfers between devices  233 us (66%)
  matrix products  54.4 us (15%)
  blocking collectives  22.5 us (6%)
  between operations  14.1 us (4%)
  other arithmetic  12.9 us (4%)
  local copies, waits for them, and re-layouts  9.09 us (3%)
    psum x1, waiting for transfers between devices, shards(): key_up_grad, value_up_grad = lax.psum((key_term, value_term), 'seq')  104 us
    ppermute x8, waiting for transfers between devices, shifted(): return lax.ppermute(value, axis, pairs)  98.6 us
    all_gather x1, blocking collectives, shards(): every_pos = lax.all_gather(positions, 'seq', axis=0, tiled=True)  22.5 us
    all_gather x1, waiting for transfers between devices, shards(): gathered = lax.all_gather(latents, 'seq', axis=0, tiled=True)  19.7 us
    dot_general x10, matrix products, up_project(): jnp.dot(compressed, value_up, preferred_element_type=jnp.float32)  12.5 us
    dot_general x10, matrix products, up_project(): jnp.dot(compressed, key_up, preferred_element_type=jnp.float32)  10.5 us
    all_gather x1, waiting for transfers between devices, shards(): latent_grad = jnp.sum(lax.all_gather(latent_part, 'head'), axis=0)  10.2 us
    dot_general x10, matrix products, scores_of(): jnp.einsum('bhd,kd->hbk', q_rope, rope_keys, preferred_element_type=jnp.f...  8.12 us
  transfers between devices with their start and end apart: 11, of which 11 were waited for; matrix products, arithmetic and copies ran while one was open for 5% of the time, Pallas kernels for 0%

profile of v1, /device:TPU:0, one launch (start us, length us, event | category | flops | bytes accessed | tf_op | source)
XLA Modules:
  0.0 349.9 jit_solution(1629887168160353393)
XLA Ops:
  8.1 1.0 copy.104
  9.1 1.1 copy.103
  10.2 22.5 %all-gather.1 = s32[8,1,128]{2,1,0:T(1,128)S(1)} all-gather(s32[1,1,128]{2,1,0:T(1,128)} %bitcast.259), channel_id=1, replica_groups=mesh['seq'=8,'head'=4] {'seq'}, dimensions={0}, use_global_device_ids=true | all-gather | bytes 4608 | tf_op jit(solution)/shard_map/all_gather | solution.py:85
  33.5 19.7 %all-gather.5.cloned.1.call-done = bf16[1024,576]{0,1:T(8,128)(2,1)} async-done(((bf16[128,576]{0,1:T(8,128)(2,1)}), bf16[1024,576]{0,1:T(8,128)(2,1)}) %all-gather.5.cloned.1.call-update) | async-done | bytes 1179664 | tf_op jit(solution)/shard_map/all_gather | solution.py:116
  53.2 1.4 convolution_convert_fusion.5
  54.8 7.6 %while.36 = (s32[]{:T(128)}, f32[4,128]{1,0:T(4,128)S(1)}, f32[4,128]{1,0:T(4,128)S(1)}, f32[4,128]{1,0:T(4,128)S(1)}, s32[1024]{0:T(1024)S(1)}, /*index=5*/s32[...) while((s32[]{:T(128)}, f32[4,128]{1,0:T(4,128)S(1)}, ...), condition=%wide.region_4.5_spmd.clone, body=%wide.region_0.4_spmd.clone.sunk | while | flops 708120064 | bytes 14854930 | solution.py:124
  55.0 1.6 convolution_convert_fusion.10
  58.8 1.6 convolution_convert_fusion.10
  62.4 0.9 convolution_bitcast_fusion.12
  63.8 1.2 fusion.47
  66.3 135.5 %while.37 = (s32[]{:T(128)}, f32[128,1088]{0,1:T(8,128)S(1)}, f32[128,768]{0,1:T(8,128)S(1)}, s32[]{:T(128)}, s32[1024]{0:T(1024)S(1)}, /*index=5*/s32[128]{0:T(...) while((s32[]{:T(128)}, f32[128,1088]{0,1:T(8,128)S(1)}, ...), condition=%wide.region_6.7_spmd.clone, body=%wide.region_5.6_spmd.clone.sunk | while | flops 244719632 | bytes 11737526 | solution.py:135
  66.4 1.2 fusion.162
  67.6 1.2 convolution_convert_fusion.11
  69.0 0.9 convolution_bitcast_fusion.21
  71.8 1.4 collective-permute-start
  74.4 12.3 %collective-permute-done = f32[128,1088]{0,1:T(8,128)S(1)} collective-permute-done((f32[128,1088]{0,1:T(8,128)}, f32[128,1088]{0,1:T(8,128)S(1)}, u32[]{:S(2)}, u32[]{:S(2)}) %collective-permute-start) | collective-permute-done | bytes 557088 | tf_op jit(solution)/shard_map/while/body/eval_jaxpr/ppermute | solution.py:17
  86.7 1.2 fusion.162
  87.9 1.2 convolution_convert_fusion.11
  89.3 0.9 convolution_bitcast_fusion.21
  92.1 1.2 collective-permute-start
  94.5 12.9 %collective-permute-done = f32[128,1088]{0,1:T(8,128)S(1)} collective-permute-done((f32[128,1088]{0,1:T(8,128)}, f32[128,1088]{0,1:T(8,128)S(1)}, u32[]{:S(2)}, u32[]{:S(2)}) %collective-permute-start) | collective-permute-done | bytes 557088 | tf_op jit(solution)/shard_map/while/body/eval_jaxpr/ppermute | solution.py:17
  107.5 1.2 fusion.162
  108.6 1.2 convolution_convert_fusion.11
  110.0 0.9 convolution_bitcast_fusion.21
  114.0 13.2 %collective-permute-done = f32[128,1088]{0,1:T(8,128)S(1)} collective-permute-done((f32[128,1088]{0,1:T(8,128)}, f32[128,1088]{0,1:T(8,128)S(1)}, u32[]{:S(2)}, u32[]{:S(2)}) %collective-permute-start) | collective-permute-done | bytes 557088 | tf_op jit(solution)/shard_map/while/body/eval_jaxpr/ppermute | solution.py:17
  127.3 1.2 fusion.162
  128.5 1.2 convolution_convert_fusion.11
  129.9 0.9 convolution_bitcast_fusion.21
  133.9 12.3 %collective-permute-done = f32[128,1088]{0,1:T(8,128)S(1)} collective-permute-done((f32[128,1088]{0,1:T(8,128)}, f32[128,1088]{0,1:T(8,128)S(1)}, u32[]{:S(2)}, u32[]{:S(2)}) %collective-permute-start) | collective-permute-done | bytes 557088 | tf_op jit(solution)/shard_map/while/body/eval_jaxpr/ppermute | solution.py:17
  146.3 1.2 fusion.162
  147.5 1.2 convolution_convert_fusion.11
  148.9 0.9 convolution_bitcast_fusion.21
  152.9 11.5 %collective-permute-done = f32[128,1088]{0,1:T(8,128)S(1)} collective-permute-done((f32[128,1088]{0,1:T(8,128)}, f32[128,1088]{0,1:T(8,128)S(1)}, u32[]{:S(2)}, u32[]{:S(2)}) %collective-permute-start) | collective-permute-done | bytes 557088 | tf_op jit(solution)/shard_map/while/body/eval_jaxpr/ppermute | solution.py:17
  164.5 1.2 fusion.162
  165.6 1.2 convolution_convert_fusion.11
  171.0 11.3 %collective-permute-done = f32[128,1088]{0,1:T(8,128)S(1)} collective-permute-done((f32[128,1088]{0,1:T(8,128)}, f32[128,1088]{0,1:T(8,128)S(1)}, u32[]{:S(2)}, u32[]{:S(2)}) %collective-permute-start) | collective-permute-done | bytes 557088 | tf_op jit(solution)/shard_map/while/body/eval_jaxpr/ppermute | solution.py:17
  182.4 1.2 fusion.162
  183.5 1.2 convolution_convert_fusion.11
  189.0 12.8 %collective-permute-done = f32[128,1088]{0,1:T(8,128)S(1)} collective-permute-done((f32[128,1088]{0,1:T(8,128)}, f32[128,1088]{0,1:T(8,128)S(1)}, u32[]{:S(2)}, u32[]{:S(2)}) %collective-permute-start) | collective-permute-done | bytes 557088 | tf_op jit(solution)/shard_map/while/body/eval_jaxpr/ppermute | solution.py:17
  201.8 1.0 maximum_add_fusion.1
  202.8 12.2 %collective-permute-done.1 = f32[128,1088]{0,1:T(8,128)S(1)} collective-permute-done((f32[128,1088]{0,1:T(8,128)S(1)}, f32[128,1088]{0,1:T(8,128)S(1)}, u32[]{:S(2)}, u32[]{:S(2)}) %collective-permute-start.1) | collective-permute-done | bytes 557088 | tf_op jit(solution)/shard_map/ppermute | solution.py:17
  217.4 1.6 convolution_bitcast_fusion.9
  219.0 1.6 convolution_bitcast_fusion.8
  222.7 10.2 %all-gather.7.cloned.1.call-done = f32[512,576]{1,0:T(8,128)} async-done(((f32[128,576]{1,0:T(8,128)}), f32[512,576]{1,0:T(8,128)}) %all-gather.7.cloned.1.call-update) | async-done | bytes 1179664 | tf_op jit(solution)/shard_map/all_gather | solution.py:150
  232.9 1.4 reduce_sum.35
  235.2 104.3 %all-reduce.3.cloned.1.call-done = (f32[512,512]{0,1:T(8,128)}, f32[512,512]{0,1:T(8,128)}) async-done(((f32[512,512]{0,1:T(8,128)}, f32[512,512]{0,1:T(8,128)}), (f32[512,512]{0,1:T(8,128)}, f32[512,512]{0,1:T(8,128)})) %all-reduce.3.cloned.1.call-update) | async-done | bytes 2097168 | tf_op jit(solution)/shard_map/psum | solution.py:155
  339.5 2.6 copy.122
  342.1 1.3 copy.123
  (167 shorter events, 38.1 us)
Async XLA Ops:
  7.2 47.6 %copy-start.5 = (bf16[128,512]{1,0:T(8,128)(2,1)S(1)}, bf16[128,512]{1,0:T(8,128)(2,1)}, u32[]{:S(2)}) copy-start(bf16[128,512]{1,0:T(8,128)(2,1)} %param.14) | copy-start | bytes 393220
  7.2 47.6 %copy-start.6 = (s32[128]{0:T(128)S(1)}, s32[128]{0:T(128)}, u32[]{:S(2)}) copy-start(s32[128]{0:T(128)} %param.15) | copy-start | bytes 1540
  7.2 47.6 %copy-start.1 = (bf16[512,512]{1,0:T(8,128)(2,1)S(1)}, bf16[512,512]{1,0:T(8,128)(2,1)}, u32[]{:S(2)}) copy-start(bf16[512,512]{1,0:T(8,128)(2,1)} %param.12) | copy-start | bytes 1572868
  7.2 47.6 %copy-start = (bf16[512,512]{1,0:T(8,128)(2,1)S(1)}, bf16[512,512]{1,0:T(8,128)(2,1)}, u32[]{:S(2)}) copy-start(bf16[512,512]{1,0:T(8,128)(2,1)} %param.13) | copy-start | bytes 1572868
  7.2 46.0 %all-gather.5.cloned.1.call-start = ((), (), s32[]{:S(2)}) async-start(), calls=%async_computation | async-start | bytes 1327104 | tf_op jit(solution)/shard_map/all_gather | solution.py:116
  7.9 225.0 %all-gather.7.cloned.1.call-start = ((), (), s32[]{:S(2)}) async-start(), calls=%async_computation.1 | async-start | bytes 1638400 | tf_op jit(solution)/shard_map/all_gather | solution.py:150
  54.8 1.9 copy-start.2
  58.6 1.9 copy-start.2
  71.8 14.8 %collective-permute-start = (f32[128,1088]{0,1:T(8,128)}, f32[128,1088]{0,1:T(8,128)S(1)}, u32[]{:S(2)}, u32[]{:S(2)}) collective-permute-start(f32[128,1088]{0,1:T(8,128)} %maximum_add_fusion.3), channel_id=1, source_target_pairs={{0,4},{4,8},{8,12},{12,16},{16,20},{20,24},{24,28},{28,0},{1,5},{5... | collective-permute-start | bytes 1671176 | tf_op jit(solution)/shard_map/while/body/eval_jaxpr/ppermute | solution.py:17
  92.1 15.2 %collective-permute-start = (f32[128,1088]{0,1:T(8,128)}, f32[128,1088]{0,1:T(8,128)S(1)}, u32[]{:S(2)}, u32[]{:S(2)}) collective-permute-start(f32[128,1088]{0,1:T(8,128)} %maximum_add_fusion.3), channel_id=1, source_target_pairs={{0,4},{4,8},{8,12},{12,16},{16,20},{20,24},{24,28},{28,0},{1,5},{5... | collective-permute-start | bytes 1671176 | tf_op jit(solution)/shard_map/while/body/eval_jaxpr/ppermute | solution.py:17
  112.9 14.4 %collective-permute-start = (f32[128,1088]{0,1:T(8,128)}, f32[128,1088]{0,1:T(8,128)S(1)}, u32[]{:S(2)}, u32[]{:S(2)}) collective-permute-start(f32[128,1088]{0,1:T(8,128)} %maximum_add_fusion.3), channel_id=1, source_target_pairs={{0,4},{4,8},{8,12},{12,16},{16,20},{20,24},{24,28},{28,0},{1,5},{5... | collective-permute-start | bytes 1671176 | tf_op jit(solution)/shard_map/while/body/eval_jaxpr/ppermute | solution.py:17
  132.7 13.5 %collective-permute-start = (f32[128,1088]{0,1:T(8,128)}, f32[128,1088]{0,1:T(8,128)S(1)}, u32[]{:S(2)}, u32[]{:S(2)}) collective-permute-start(f32[128,1088]{0,1:T(8,128)} %maximum_add_fusion.3), channel_id=1, source_target_pairs={{0,4},{4,8},{8,12},{12,16},{16,20},{20,24},{24,28},{28,0},{1,5},{5... | collective-permute-start | bytes 1671176 | tf_op jit(solution)/shard_map/while/body/eval_jaxpr/ppermute | solution.py:17
  151.7 12.7 %collective-permute-start = (f32[128,1088]{0,1:T(8,128)}, f32[128,1088]{0,1:T(8,128)S(1)}, u32[]{:S(2)}, u32[]{:S(2)}) collective-permute-start(f32[128,1088]{0,1:T(8,128)} %maximum_add_fusion.3), channel_id=1, source_target_pairs={{0,4},{4,8},{8,12},{12,16},{16,20},{20,24},{24,28},{28,0},{1,5},{5... | collective-permute-start | bytes 1671176 | tf_op jit(solution)/shard_map/while/body/eval_jaxpr/ppermute | solution.py:17
  169.9 12.4 %collective-permute-start = (f32[128,1088]{0,1:T(8,128)}, f32[128,1088]{0,1:T(8,128)S(1)}, u32[]{:S(2)}, u32[]{:S(2)}) collective-permute-start(f32[128,1088]{0,1:T(8,128)} %maximum_add_fusion.3), channel_id=1, source_target_pairs={{0,4},{4,8},{8,12},{12,16},{16,20},{20,24},{24,28},{28,0},{1,5},{5... | collective-permute-start | bytes 1671176 | tf_op jit(solution)/shard_map/while/body/eval_jaxpr/ppermute | solution.py:17
  187.8 14.0 %collective-permute-start = (f32[128,1088]{0,1:T(8,128)}, f32[128,1088]{0,1:T(8,128)S(1)}, u32[]{:S(2)}, u32[]{:S(2)}) collective-permute-start(f32[128,1088]{0,1:T(8,128)} %maximum_add_fusion.3), channel_id=1, source_target_pairs={{0,4},{4,8},{8,12},{12,16},{16,20},{20,24},{24,28},{28,0},{1,5},{5... | collective-permute-start | bytes 1671176 | tf_op jit(solution)/shard_map/while/body/eval_jaxpr/ppermute | solution.py:17
  202.8 12.3 %collective-permute-start.1 = (f32[128,1088]{0,1:T(8,128)S(1)}, f32[128,1088]{0,1:T(8,128)S(1)}, u32[]{:S(2)}, u32[]{:S(2)}) collective-permute-start(f32[128,1088]{0,1:T(8,128)S(1)} %maximum_add_fusion.1), channel_id=1, source_target_pairs={{0,4},{4,8},{8,12},{12,16},{16,20},{20,24},{24,28},{28,0},{1,5},{5... | collective-permute-start | bytes 1671176 | tf_op jit(solution)/shard_map/ppermute | solution.py:17
  215.9 1.6 copy-start.3
  217.4 122.1 %all-reduce.3.cloned.1.call-start = ((), (), s32[]{:S(2)}) async-start(), calls=%async_computation.2 | async-start | bytes 4194304 | tf_op jit(solution)/shard_map/psum | solution.py:155
  339.5 2.6 copy-start.4
Sparse Core Ops, SparseCore 0:
  10.1 43.1 all-gather.4
  217.5 15.3 all-gather.6
  237.2 102.2 all-reduce.2
